TPU v7x, 512 devices: a whole 4x8x8 slice. The times are simulated.
512 devices in a mesh: section: 16 (over x, y_lo), dp: 32 (over z, y_hi, core).
Axes of the slice: x: 4, y: 8 (y_hi: 2, y_lo: 4; y = y_hi * 4 + y_lo), z: 8, core: 2. Of those that a mesh axis runs over, the one named last changes fastest.
Arguments:
- acts: bfloat16 [16, 4, 1024, 4096], P('section', None, 'dp'), may hold values from -6 to 6
- grads_out: bfloat16 [16, 4, 1024, 4096], P('section', None, 'dp'), may hold values from -6 to 6
- weight_grad: bfloat16 [16, 4096, 4096], P('section', 'dp'), may hold values from -16 to 16
- old_in_factor: float32 [16, 32, 128, 128], P('section', 'dp'), may hold values from -12 to 24, as said below
- old_out_factor: float32 [16, 32, 128, 128], P('section', 'dp'), may hold values from -12 to 24, as said below
Outputs:
- update: bfloat16 [16, 4096, 4096], P('section', 'dp')
- in_factor: float32 [16, 32, 128, 128], P('section', 'dp')
- out_factor: float32 [16, 32, 128, 128], P('section', 'dp')
Inputs may be any that keep to these rules, and one draw needn't show every extreme that they name: `old_in_factor`: each block is symmetric positive definite. `old_out_factor`: each block is symmetric positive definite.
All inputs are finite; a program needn't handle non-finite values.
Results may differ from a plain program's by a relative error of at most 0.0064.
Values may be sent and summed in bfloat16 or wider, within the bound.
A program may use at most 64 MiB of HBM per device.

v0:
```python
import jax
import jax.numpy as jnp
from jax import lax
from jax.sharding import Mesh
from jax.sharding import PartitionSpec as P

ITERS = 8
DP = ("dp_0", "dp_1", "dp_2")
SECTION = ("section_0", "section_1")
SECTION_DP = ("section_0", "section_1", "dp_0", "dp_1", "dp_2")


DECAY = 0.7
DAMPING = 0.1
CLIP = 0.04
HIGH = lax.Precision.HIGHEST


def in_one_piece(arrays, axis, split_dim, concat_dim, along):
    ends, at = ([], 0)
    for a in arrays[:-1]:
        at += a.shape[along]
        ends.append(at)
    both = jnp.concatenate(arrays, axis=along)
    return tuple(
        jnp.split(
            lax.all_to_all(both, axis, split_axis=split_dim, concat_axis=concat_dim, tiled=True),
            ends,
            axis=along,
        )
    )


def from_everyone(x, axis):
    devices = lax.axis_size(axis)
    return lax.all_to_all(jnp.broadcast_to(x[None], (devices, *x.shape)), axis, 0, 0, tiled=True)


def in_order(tiles, dim):
    shape = list(tiles.shape[1:])
    shape[dim] *= tiles.shape[0]
    return jnp.moveaxis(tiles, 0, dim).reshape(shape)


def gather_directly(x, axis, dim):
    tiles = from_everyone(x, axis)
    return in_order(tiles, dim)


def one_axis_at_a_time(x, axes):
    for axis in axes:
        x = lax.psum(x, axis)
    return x


def newton(factor):
    size = factor.shape[-1]
    eye = jnp.eye(size, dtype=jnp.float32)
    damped = factor + DAMPING * eye
    norms = jnp.sqrt(jnp.sum(damped * damped, axis=(1, 2)))
    approx = eye[None] / norms[:, None, None]
    for sweep in range(ITERS):
        product = jnp.einsum("bij,bjk->bik", damped, approx, precision=HIGH)
        approx = jnp.einsum("bij,bjk->bik", approx, 2.0 * eye - product, precision=HIGH)
    return approx


def block_gram(values, block, count):
    flat = values.reshape(-1, values.shape[-1] // block, block)
    return jnp.einsum("tbi,tbj->bij", flat, flat, preferred_element_type=jnp.float32) / count


def body(acts, grads_out, weight_grad, old_in_factor, old_out_factor):
    groups = lax.axis_size(DP)
    sections = lax.axis_size(SECTION)
    block = old_in_factor.shape[-1]
    width = acts.shape[3]
    count = acts.shape[1] * acts.shape[2] * groups
    moved_in, moved_out = in_one_piece((acts[0], grads_out[0]), DP, 2, 1, 0)
    gram_in = block_gram(moved_in, block, count)
    gram_out = block_gram(moved_out, block, count)
    in_factor = DECAY * old_in_factor[0] + (1.0 - DECAY) * gram_in
    out_factor = DECAY * old_out_factor[0] + (1.0 - DECAY) * gram_out
    in_inverse = newton(in_factor).astype(jnp.bfloat16)
    out_inverse = newton(out_factor).astype(jnp.bfloat16)
    rows = weight_grad.shape[1]
    grad_blocks = weight_grad[0].reshape(rows // block, block, width)
    left = jnp.einsum("bij,bjd->bid", out_inverse, grad_blocks, preferred_element_type=jnp.float32)
    left = left.astype(jnp.bfloat16).reshape(rows, width)
    split = left.reshape(rows, width // block, block)
    natural = jnp.einsum(
        "rci,cij->rcj",
        split,
        gather_directly(in_inverse, DP, 0),
        preferred_element_type=jnp.float32,
    ).reshape(rows, width)
    quad = one_axis_at_a_time(jnp.sum(natural * weight_grad[0].astype(jnp.float32)), SECTION_DP)
    numel = sections * rows * groups * width
    scale = jnp.minimum(1.0, jnp.sqrt(CLIP * numel / quad))
    update = (scale * natural).astype(jnp.bfloat16)
    return (update[None], in_factor[None], out_factor[None])


def solution(mesh):
    torus = Mesh(
        mesh.devices.reshape(4, 4, 8, 2, 2), ("section_0", "section_1", "dp_0", "dp_1", "dp_2")
    )
    in_specs = (
        P(SECTION, None, DP, None),
        P(SECTION, None, DP, None),
        P(SECTION, DP, None),
        P(SECTION, DP, None, None),
        P(SECTION, DP, None, None),
    )
    out_specs = (P(SECTION, DP, None), P(SECTION, DP, None, None), P(SECTION, DP, None, None))
    return jax.shard_map(body, mesh=torus, in_specs=in_specs, out_specs=out_specs, check_vma=False)
```

profile of v0, /device:TPU:1, one launch (start us, length us, event | category | flops | bytes accessed | tf_op | source)
XLA Modules:
  0.0 232.7 jit_solution(4203636534374139186)
XLA Ops:
  0.6 1.7 pad_maximum_fusion
  2.4 7.7 %copy.25 = bf16[8,32,4096]{1,0,2:T(8,128)(2,1)} copy(bf16[8,32,4096]{2,1,0:T(8,128)(2,1)S(1)} %pad_maximum_fusion) | data formatting | bytes 4194304 | tf_op jit(solution)/shard_map/concatenate | solution.py:24
  10.0 13.3 %reshape.280 = bf16[32,2,16384]{2,1,0:T(2,128)(2,1)} reshape(bf16[4096,8,32]{2,1,0:T(8,128)(2,1)} %bitcast.99) | data formatting | bytes 4194304
  23.3 17.4 %all-to-all-start = ((bf16[32,2,16384]{2,1,0:T(2,128)(2,1)}), bf16[32,2,16384]{2,1,0:T(2,128)(2,1)}, u32[]{:S(2)}, u32[]{:S(2)}) async-start(bf16[32,2,16384]{2,1,0:T(2,128)(2,1)} %reshape.280), calls=%async_computation | async-start | bytes 4194304 | tf_op jit(solution)/shard_map/all_to_all | solution.py:27
  40.8 0.5 copy.30
  41.3 56.0 %all-to-all-done = bf16[32,2,16384]{2,1,0:T(2,128)(2,1)} async-done(((bf16[32,2,16384]{2,1,0:T(2,128)(2,1)}), bf16[32,2,16384]{2,1,0:T(2,128)(2,1)}, u32[]{:S(2)}, u32[]{:S(2)}) %all-to-all-start) | async-done | bytes 2097184 | tf_op jit(solution)/shard_map/all_to_all | solution.py:27
  97.3 11.7 %reshape.281 = bf16[4096,8,32]{2,1,0:T(8,128)(2,1)} reshape(bf16[32,2,16384]{2,1,0:T(2,128)(2,1)} %all-to-all-done) | data formatting | bytes 4194304
  109.0 9.4 %copy.27 = bf16[8,32,32,128]{3,1,2,0:T(8,128)(2,1)} copy(bf16[8,32,32,128]{1,0,3,2:T(8,128)(2,1)} %bitcast.100) | data formatting | bytes 4194304 | tf_op jit(solution)/shard_map/all_to_all | solution.py:27
  118.4 2.8 %multiply_reduce_fusion.1 = (f32[]{:T(128)}, f32[128,128]{1,0:T(8,128)S(1)}) fusion(bf16[8,32,32,128]{3,2,1,0:T(8,128)(2,1)} %bitcast.105, f32[1,1,128,128]{3,2,1,0:T(8,128)S(1)} %copy-done.3), kind=kOutput, calls=%fused_computation.47 | convolution fusion | flops 134348800 | bytes 3276804 | tf_op jit(solution)/shard_map/tbi,tbj->bij/dot_general | solution.py:70
  121.9 0.2 convolution_subtract_fusion.15
  122.1 0.2 fusion.17
  122.3 0.2 convolution_subtract_fusion.14
  122.5 0.2 fusion.32
  122.7 0.2 convolution_subtract_fusion.13
  122.9 0.2 fusion.33
  123.2 0.2 convolution_subtract_fusion.12
  123.4 0.2 fusion.34
  123.6 0.2 convolution_subtract_fusion.11
  124.0 0.2 convolution_subtract_fusion.10
  124.2 0.2 fusion.36
  124.4 0.2 convolution_subtract_fusion.9
  124.9 0.2 convolution_subtract_fusion.8
  125.1 0.2 convolution_convert_fusion.2
  125.4 1.2 broadcast_in_dim.6
  126.6 9.7 %all-to-all-start.1 = ((bf16[32,1,128,128]{2,3,1,0:T(8,128)(2,1)}), bf16[32,1,128,128]{2,3,1,0:T(8,128)(2,1)}, u32[]{:S(2)}, u32[]{:S(2)}) async-start(bf16[32,1,128,128]{2,3,1,0:T(8,128)(2,1)} %broadcast_in_dim.6), calls=%async_computation.1 | async-start | bytes 2097152 | tf_op jit(solution)/shard_map/all_to_all | solution.py:36
  136.4 2.6 %multiply_reduce_fusion = (f32[]{:T(128)}, f32[128,128]{1,0:T(8,128)S(1)}) fusion(bf16[8,32,32,128]{3,2,1,0:T(8,128)(2,1)} %bitcast.106, f32[1,1,128,128]{3,2,1,0:T(8,128)S(1)} %copy-done.4), kind=kOutput, calls=%fused_computation.46 | convolution fusion | flops 134348800 | bytes 3276804 | tf_op jit(solution)/shard_map/tbi,tbj->bij/dot_general | solution.py:70
  139.7 0.2 convolution_subtract_fusion.7
  139.9 0.2 fusion.14
  140.1 0.2 convolution_subtract_fusion.6
  140.6 0.2 convolution_subtract_fusion.5
  140.8 0.2 fusion.39
  141.0 0.2 convolution_subtract_fusion.4
  141.4 0.2 convolution_subtract_fusion.3
  141.8 0.2 convolution_subtract_fusion.2
  142.0 0.2 fusion.42
  142.3 0.2 convolution_subtract_fusion.1
  142.7 0.2 convolution_subtract_fusion
  142.9 0.2 convolution_convert_fusion.1
  143.1 1.4 fusion.2
  144.5 20.4 %all-to-all-done.1 = bf16[32,1,128,128]{2,3,1,0:T(8,128)(2,1)} async-done(((bf16[32,1,128,128]{2,3,1,0:T(8,128)(2,1)}), bf16[32,1,128,128]{2,3,1,0:T(8,128)(2,1)}, u32[]{:S(2)}, u32[]{:S(2)}) %all-to-all-start.1) | async-done | bytes 1048608 | tf_op jit(solution)/shard_map/all_to_all | solution.py:36
  164.9 4.3 %fusion = (f32[]{:T(128)}, f32[32,128,128]{2,1,0:T(8,128)}) fusion(f32[128,32,128]{0,2,1:T(8,128)S(1)} %bitcast.101, bf16[16,32,8,128]{3,2,1,0:T(8,128)(2,1)} %fusion.2, bf16[32,1,128,128]{2,3,1,0:T(8,128)(2,1)} %all-to-all-done.1), kind=kOutput, calls=%fused_computation.4 | convolution fusion | flops 135266304 | bytes 6291460 | tf_op jit(solution)/shard_map/rci,cij->rcj/dot_general | solution.py:91
  169.2 9.1 %psum.35 = f32[]{:T(128)} all-reduce(f32[]{:T(128)} %get-tuple-element.19), channel_id=1, replica_groups=mesh['section_0'=4,'section_1'=4,'dp_0'=8,'dp_1'=2,'dp_2'=2] {'section_0'}, use_global_device_ids=true, to_apply=%region_3.0 | all-reduce | flops 1 | bytes 8 | tf_op jit(solution)/shard_map/psum | solution.py:52
  178.2 15.8 %psum.36 = f32[]{:T(128)} all-reduce(f32[]{:T(128)} %psum.35), channel_id=1, replica_groups=mesh['section_0'=4,'section_1'=4,'dp_0'=8,'dp_1'=2,'dp_2'=2] {'section_1'}, use_global_device_ids=true, to_apply=%region_4.0 | all-reduce | flops 1 | bytes 8 | tf_op jit(solution)/shard_map/psum | solution.py:52
  194.0 13.3 %psum.37 = f32[]{:T(128)} all-reduce(f32[]{:T(128)} %psum.36), channel_id=1, replica_groups=mesh['section_0'=4,'section_1'=4,'dp_0'=8,'dp_1'=2,'dp_2'=2] {'dp_0'}, use_global_device_ids=true, to_apply=%region_5.0 | all-reduce | flops 1 | bytes 8 | tf_op jit(solution)/shard_map/psum | solution.py:52
  207.4 8.3 %psum.38 = f32[]{:T(128)} all-reduce(f32[]{:T(128)} %psum.37), channel_id=1, replica_groups=mesh['section_0'=4,'section_1'=4,'dp_0'=8,'dp_1'=2,'dp_2'=2] {'dp_1'}, use_global_device_ids=true, to_apply=%region_6.0 | all-reduce | flops 1 | bytes 8 | tf_op jit(solution)/shard_map/psum | solution.py:52
  215.7 13.1 %psum.39 = f32[]{:T(128)} all-reduce(f32[]{:T(128)} %psum.38), channel_id=1, replica_groups=mesh['section_0'=4,'section_1'=4,'dp_0'=8,'dp_1'=2,'dp_2'=2] {'dp_2'}, use_global_device_ids=true, to_apply=%region_7.0 | all-reduce | flops 1 | bytes 8 | tf_op jit(solution)/shard_map/psum | solution.py:52
  229.5 1.9 fusion.1
  231.4 1.3 copy.31
  (17 shorter events, 1.3 us)
Async XLA Ops:
  23.3 17.4 %copy-start = (bf16[1,128,4096]{2,1,0:T(8,128)(2,1)S(1)}, bf16[1,128,4096]{2,1,0:T(8,128)(2,1)}, u32[]{:S(2)}) copy-start(bf16[1,128,4096]{2,1,0:T(8,128)(2,1)} %param.7) | copy-start | bytes 3145732
  23.3 73.9 %all-to-all-start = ((bf16[32,2,16384]{2,1,0:T(2,128)(2,1)}), bf16[32,2,16384]{2,1,0:T(2,128)(2,1)}, u32[]{:S(2)}, u32[]{:S(2)}) async-start(bf16[32,2,16384]{2,1,0:T(2,128)(2,1)} %reshape.280), calls=%async_computation | async-start | bytes 4194304 | tf_op jit(solution)/shard_map/all_to_all | solution.py:27
  109.0 9.4 %copy-start.3 = (f32[1,1,128,128]{3,2,1,0:T(8,128)S(1)}, f32[1,1,128,128]{3,2,1,0:T(8,128)}, u32[]{:S(2)}) copy-start(f32[1,1,128,128]{3,2,1,0:T(8,128)} %param.8) | copy-start | bytes 196612
  121.2 5.5 %copy-start.1 = (f32[128,128]{1,0:T(8,128)}, f32[128,128]{1,0:T(8,128)S(1)}, u32[]{:S(2)}) copy-start(f32[128,128]{1,0:T(8,128)S(1)} %get-tuple-element.18) | copy-start | bytes 196612
  124.2 12.2 %copy-start.4 = (f32[1,1,128,128]{3,2,1,0:T(8,128)S(1)}, f32[1,1,128,128]{3,2,1,0:T(8,128)}, u32[]{:S(2)}) copy-start(f32[1,1,128,128]{3,2,1,0:T(8,128)} %param.9) | copy-start | bytes 196612
  126.6 38.2 %all-to-all-start.1 = ((bf16[32,1,128,128]{2,3,1,0:T(8,128)(2,1)}), bf16[32,1,128,128]{2,3,1,0:T(8,128)(2,1)}, u32[]{:S(2)}, u32[]{:S(2)}) async-start(bf16[32,1,128,128]{2,3,1,0:T(8,128)(2,1)} %broadcast_in_dim.6), calls=%async_computation.1 | async-start | bytes 2097152 | tf_op jit(solution)/shard_map/all_to_all | solution.py:36
  139.0 5.5 %copy-start.2 = (f32[128,128]{1,0:T(8,128)}, f32[128,128]{1,0:T(8,128)S(1)}, u32[]{:S(2)}) copy-start(f32[128,128]{1,0:T(8,128)S(1)} %get-tuple-element.16) | copy-start | bytes 196612
where the time goes:
time: 234 us; the launch traced here: 233 us
  waiting for transfers between devices  76.3 us (33%)
  blocking collectives  59.6 us (25%)
  local copies, waits for them, and re-layouts  45.3 us (19%)
  starting transfers between devices  27.1 us (12%)
  matrix products  17.7 us (8%)
  other arithmetic  3.6 us (2%)
  between operations  3.07 us (1%)
    psum x5, blocking collectives, one_axis_at_a_time(): x = lax.psum(x, axis)  59.6 us
    all_to_all x1, waiting for transfers between devices, in_one_piece(): lax.all_to_all(both, axis, split_axis=split_dim, concat_axis=concat_dim,...  56 us
    unnamed x13, local copies, waits for them, and re-layouts  26.4 us
    all_to_all x1, waiting for transfers between devices, from_everyone(): lax.all_to_all(jnp.broadcast_to(x[None], (devices, *x.shape)), axis, 0, 0...  20.4 us
    all_to_all x1, starting transfers between devices, in_one_piece(): lax.all_to_all(both, axis, split_axis=split_dim, concat_axis=concat_dim,...  17.4 us
    all_to_all x1, starting transfers between devices, from_everyone(): lax.all_to_all(jnp.broadcast_to(x[None], (devices, *x.shape)), axis, 0, 0...  9.72 us
    all_to_all x1, local copies, waits for them, and re-layouts, in_one_piece(): lax.all_to_all(both, axis, split_axis=split_dim, concat_axis=concat_dim,...  9.38 us
    concatenate x1, local copies, waits for them, and re-layouts, in_one_piece(): both = jnp.concatenate(arrays, axis=along)  7.67 us
  transfers between devices with their start and end apart: 2, of which 2 were waited for; matrix products, arithmetic and copies ran while one was open for 3% of the time, Pallas kernels for 0%

commit v1 on v0

v1 whole, which is shorter than its diff:
```python
import jax
import jax.numpy as jnp
from jax import lax
from jax.experimental import pallas as pl
from jax.experimental.pallas import tpu as pltpu
from jax.sharding import Mesh
from jax.sharding import PartitionSpec as P

ITERS = 8
SECTION = ("section_0", "section_1")
DP = ("dp_0", "dp_1", "dp_2")
DECAY = 0.7
DAMPING = 0.1
CLIP = 0.04
HIGH = lax.Precision.HIGHEST
MESH_ID = pl.DeviceIdType.MESH

X, YL, Z, YH, CORE = 4, 4, 8, 2, 2
CHIPS = Z * YH
B = 128
H = B // 2
ROWS = H + 8
F32 = jnp.float32
BF16 = jnp.bfloat16


def iotas():
    return (
        lax.broadcasted_iota(jnp.int32, (H, B), 0),
        lax.broadcasted_iota(jnp.int32, (H, B), 1),
    )


def pack(full):
    r, l = iotas()
    top, low = full[:H], pltpu.roll(full[H:], H, 1)
    body = jnp.where((l < H) & (r > l), low, top)
    diag = jnp.sum(jnp.where(r == l, low, 0.0), axis=0, keepdims=True)
    return body, jnp.broadcast_to(diag, (8, B))


def unpack(packed):
    r, l = iotas()
    body, diag = packed[:H], packed[H : H + 1]
    turned = jnp.concatenate([body, jnp.zeros((H, B), F32)], axis=0).T
    left_t, right_t = turned[:H], turned[H:]
    top = jnp.where((l < H) & (r > l), left_t, body)
    corner = jnp.where(r > l, body, jnp.where(r == l, diag, left_t))
    bottom = jnp.where(l < H, right_t, pltpu.roll(corner, H, 1))
    return jnp.concatenate([top, bottom], axis=0)


def eye():
    return (
        lax.broadcasted_iota(jnp.int32, (B, B), 0) == lax.broadcasted_iota(jnp.int32, (B, B), 1)
    ).astype(F32)


def dot(a, b):
    return jnp.dot(a, b, precision=HIGH, preferred_element_type=F32)


def newton(factor):
    one = eye()
    damped = factor + DAMPING * one
    inv = 1.0 / jnp.sqrt(jnp.sum(damped * damped, keepdims=True))
    rest = one - inv * damped
    approx = inv * (one + rest)
    rest = dot(rest, rest)
    for _ in range(ITERS - 2):
        both = dot(rest, jnp.concatenate([rest, approx], axis=1))
        approx = approx + both[:, B:]
        rest = both[:, :B]
    return approx + dot(rest, approx)


def offsets(i):
    j = i // 2
    dz = 4 + ((j + 1) // 2) * (1 - 2 * (j % 2))
    return dz, 1 - i % 2


def kernel(
    acts, grads, wgrad, old_in, old_out,
    nat_o, fin_o, fout_o, scale_o,
    tok_in, tok_out, wv, oi, oo, fi, fo,
    pk_in, pk_out, own_in, own_out, d2d_in, d2d_out,
    comb_in, comb_out, rx_in, rx_out,
    xall, left, nat, q1, q2, mine, mine2,
    ld, st, d_s, d_r, a_s, a_r, g_s, g_r, f_s, f_r, s1, r1, s2, r2,
):
    x, yl = lax.axis_index("section_0"), lax.axis_index("section_1")
    z, yh, c = lax.axis_index("dp_0"), lax.axis_index("dp_1"), lax.axis_index("dp_2")
    q_me = z * YH + yh
    other = {"dp_2": 1 - c}

    loads = [
        pltpu.make_async_copy(acts.at[0], tok_in, ld.at[0]),
        pltpu.make_async_copy(grads.at[0], tok_out, ld.at[1]),
        pltpu.make_async_copy(old_in.at[0, 0], oi, ld.at[2]),
        pltpu.make_async_copy(old_out.at[0, 0], oo, ld.at[3]),
        pltpu.make_async_copy(wgrad.at[0], wv, ld.at[4]),
    ]
    for copy in loads:
        copy.start()

    def chip_to(i):
        dz, dy = offsets(i)
        return (z + dz) % Z, (yh + dy) % YH

    def chip_from(i):
        dz, dy = offsets(i)
        return (z + Z - dz) % Z, (yh + dy) % YH

    def plane_to(k):
        y = (yh * YL + yl + k % 8) % 8
        return {"section_0": (x + k // 8) % X, "section_1": y % YL, "dp_1": y // YL}

    def column_to(k):
        return {"dp_0": (z + k // 2) % Z, "dp_2": (c + k % 2) % CORE}

    barrier = pltpu.get_barrier_semaphore()
    pl.semaphore_signal(barrier, inc=1, device_id=other, device_id_type=MESH_ID)

    @pl.loop(0, CHIPS - 1)
    def _(i):
        tz, ty = chip_to(i)
        pl.semaphore_signal(
            barrier, inc=1, device_id={"dp_0": tz, "dp_1": ty}, device_id_type=MESH_ID
        )

    @pl.loop(1, X * 8)
    def _(k):
        @pl.when(k != 4)
        def _():
            pl.semaphore_signal(barrier, inc=1, device_id=plane_to(k), device_id_type=MESH_ID)

    @pl.loop(1, Z)
    def _(k):
        pl.semaphore_signal(
            barrier, inc=1, device_id=column_to(2 * k + 1), device_id_type=MESH_ID
        )

    def gram(tok, p, core):
        at = pl.multiple_of((p * CORE + core) * B, B)
        t = tok[:, :, pl.ds(at, B)].reshape(B, B)
        return lax.dot_general(t, t, (((0,), (0,)), ((), ())), preferred_element_type=F32)

    def for_partner(tok, out):
        @pl.loop(0, CHIPS)
        def _(p):
            body, diag = pack(gram(tok, p, 1 - c))
            out[p, :H] = body.astype(BF16)
            out[p, H:] = diag.astype(BF16)

    def for_me(tok, out):
        @pl.loop(0, CHIPS)
        def _(p):
            body, diag = pack(gram(tok, p, c))
            out[p, :H] = body
            out[p, H:] = diag

    def to_partner(kind, src, dst):
        return pltpu.make_async_remote_copy(
            src_ref=src, dst_ref=dst, send_sem=d_s.at[kind], recv_sem=d_r.at[kind],
            device_id=other, device_id_type=MESH_ID,
        )

    def exchange(kind, src, dst, i, slot_from, slot_to, tz, ty):
        return pltpu.make_async_remote_copy(
            src_ref=src.at[slot_from], dst_ref=dst.at[slot_to],
            send_sem=a_s.at[kind, i], recv_sem=a_r.at[kind, slot_to],
            device_id={"dp_0": tz, "dp_1": ty}, device_id_type=MESH_ID,
        )

    def combine(kind, own, got, comb, rx):
        @pl.loop(0, CHIPS - 1)
        def _(i):
            tz, ty = chip_to(i)
            q = tz * YH + ty
            comb[q] = (own[q] + got[q].astype(F32)).astype(BF16)
            exchange(kind, comb, rx, i, q, q_me, tz, ty).start()

    def collect(kind, own, got, comb, rx):
        acc = own[q_me] + got[q_me].astype(F32)

        def step(i, acc):
            fz, fy = chip_from(CHIPS - 2 - i)
            q = fz * YH + fy
            exchange(kind, comb, rx, CHIPS - 2 - i, q, q, fz, fy).wait_recv()
            return acc + rx[q].astype(F32)

        return lax.fori_loop(0, CHIPS - 1, step, acc)

    count = F32(4.0 * 32 * Z * YH * CORE)

    loads[0].wait()
    for_partner(tok_in, pk_in)
    for_me(tok_in, own_in)
    pl.semaphore_wait(barrier, 1 + (CHIPS - 1) + (X * 8 - 2) + (Z - 1))
    in_pair = to_partner(0, pk_in, d2d_in)
    in_pair.start()
    loads[1].wait()
    for_partner(tok_out, pk_out)
    out_pair = to_partner(1, pk_out, d2d_out)
    out_pair.start()
    in_pair.wait_recv()
    combine(0, own_in, d2d_in, comb_in, rx_in)
    for_me(tok_out, own_out)
    out_pair.wait_recv()
    combine(1, own_out, d2d_out, comb_out, rx_out)
    for copy in loads[2:]:
        copy.wait()

    gram_in = unpack(collect(0, own_in, d2d_in, comb_in, rx_in))
    in_factor = DECAY * oi[...] + ((1.0 - DECAY) / count) * gram_in
    fi[...] = in_factor
    body, diag = pack(newton(in_factor))
    b_me = q_me * CORE + c
    xall[b_me, :H] = body.astype(BF16)
    xall[b_me, H:] = diag.astype(BF16)

    def gather(i, slot, q, tz, ty):
        return pltpu.make_async_remote_copy(
            src_ref=xall.at[slot], dst_ref=xall.at[slot],
            send_sem=g_s.at[i], recv_sem=g_r.at[q],
            device_id={"dp_0": tz, "dp_1": ty}, device_id_type=MESH_ID,
        )

    def forward(slot, q):
        return pltpu.make_async_remote_copy(
            src_ref=xall.at[slot], dst_ref=xall.at[slot],
            send_sem=f_s.at[q], recv_sem=f_r.at[q],
            device_id=other, device_id_type=MESH_ID,
        )

    forward(b_me, q_me).start()

    @pl.loop(0, CHIPS - 1)
    def _(i):
        tz, ty = chip_to(i)
        gather(i, b_me, q_me, tz, ty).start()

    save_in = pltpu.make_async_copy(fi, fin_o.at[0, 0], st.at[0])
    save_in.start()

    gram_out = unpack(collect(1, own_out, d2d_out, comb_out, rx_out))
    out_factor = DECAY * oo[...] + ((1.0 - DECAY) / count) * gram_out
    fo[...] = out_factor
    out_inverse = newton(out_factor).astype(BF16)
    save_out = pltpu.make_async_copy(fo, fout_o.at[0, 0], st.at[1])
    save_out.start()

    @pl.loop(0, 8)
    def _(k):
        at = pl.ds(pl.multiple_of(k * 512, 512), 512)
        left[:, at] = jnp.dot(out_inverse, wv[:, at], preferred_element_type=F32).astype(BF16)

    def block(slot, acc):
        inverse = unpack(xall[slot].astype(F32)).astype(BF16)
        at = pl.ds(pl.multiple_of(slot * B, B), B)
        part = jnp.dot(left[:, at], inverse, preferred_element_type=F32)
        nat[:, at] = part
        part = part * wv[:, at].astype(F32)
        return acc + jnp.sum(part.reshape(16, 8, B), axis=0)

    acc = block(b_me, jnp.zeros((8, B), F32))
    forward(b_me, q_me).wait_recv()
    acc = block(q_me * CORE + 1 - c, acc)

    def arrive(k, acc):
        i = CHIPS - 2 - k
        fz, fy = chip_from(i)
        q = fz * YH + fy
        slot = q * CORE + c
        gather(i, slot, q, fz, fy).wait_recv()
        forward(slot, q).start()
        acc = block(slot, acc)
        forward(slot, q).wait_recv()
        return block(q * CORE + 1 - c, acc)

    acc = lax.fori_loop(0, CHIPS - 1, arrive, acc)
    save_nat = pltpu.make_async_copy(nat, nat_o, st.at[2])
    save_nat.start()

    total = jnp.sum(acc)
    mine[...] = jnp.full((1, B), total, F32)

    def plane(k, slot):
        return pltpu.make_async_remote_copy(
            src_ref=mine, dst_ref=q1.at[slot], send_sem=s1.at[k], recv_sem=r1.at[slot],
            device_id=plane_to(k), device_id_type=MESH_ID,
        )

    def column(k, slot):
        return pltpu.make_async_remote_copy(
            src_ref=mine2, dst_ref=q2.at[slot], send_sem=s2.at[k], recv_sem=r2.at[slot],
            device_id=column_to(k), device_id_type=MESH_ID,
        )

    @pl.loop(1, X * 8)
    def _(k):
        plane(k, k).start()

    quad = mine[...]

    def plane_sum(k, quad):
        plane(k, k).wait_recv()
        return quad + q1[k]

    quad = lax.fori_loop(1, X * 8, plane_sum, quad)
    mine2[...] = quad

    @pl.loop(1, Z * CORE)
    def _(k):
        column(k, k).start()

    def column_sum(k, quad):
        column(k, k).wait_recv()
        return quad + q2[k]

    quad = lax.fori_loop(1, Z * CORE, column_sum, quad)
    numel = F32(X * YL * 4096.0 * 4096.0)
    scale_o[...] = jnp.minimum(1.0, jnp.sqrt(CLIP * numel / quad))

    in_pair.wait_send()
    out_pair.wait_send()
    forward(b_me, q_me).wait_send()

    @pl.loop(0, CHIPS - 1)
    def _(i):
        tz, ty = chip_to(i)
        exchange(0, comb_in, rx_in, i, 0, 0, tz, ty).wait_send()
        exchange(1, comb_out, rx_out, i, 0, 0, tz, ty).wait_send()
        gather(i, b_me, q_me, tz, ty).wait_send()
        q = tz * YH + ty
        forward(q * CORE + c, q).wait_send()

    @pl.loop(1, X * 8)
    def _(k):
        plane(k, k).wait_send()

    @pl.loop(1, Z * CORE)
    def _(k):
        column(k, k).wait_send()

    save_in.wait()
    save_out.wait()
    save_nat.wait()


def body(acts, grads_out, weight_grad, old_in_factor, old_out_factor):
    rows, width = weight_grad.shape[1:]
    any_space = pl.BlockSpec(memory_space=pl.ANY)
    dma = pltpu.SemaphoreType.DMA
    vmem = pltpu.VMEM
    packed = (CHIPS, ROWS, B)
    nat, in_factor, out_factor, scale = pl.pallas_call(
        kernel,
        out_shape=(
            jax.ShapeDtypeStruct((rows, width), F32),
            jax.ShapeDtypeStruct(old_in_factor.shape, F32),
            jax.ShapeDtypeStruct(old_out_factor.shape, F32),
            jax.ShapeDtypeStruct((1, B), F32),
        ),
        in_specs=[any_space] * 5,
        out_specs=(any_space, any_space, any_space, pl.BlockSpec(memory_space=vmem)),
        scratch_shapes=[
            vmem(acts.shape[1:], BF16),
            vmem(acts.shape[1:], BF16),
            vmem((rows, width), BF16),
            vmem((B, B), F32),
            vmem((B, B), F32),
            vmem((B, B), F32),
            vmem((B, B), F32),
            vmem(packed, BF16),
            vmem(packed, BF16),
            vmem(packed, F32),
            vmem(packed, F32),
            vmem(packed, BF16),
            vmem(packed, BF16),
            vmem(packed, BF16),
            vmem(packed, BF16),
            vmem(packed, BF16),
            vmem(packed, BF16),
            vmem((CHIPS * CORE, ROWS, B), BF16),
            vmem((rows, width), BF16),
            vmem((rows, width), F32),
            vmem((X * 8, 1, B), F32),
            vmem((Z * CORE, 1, B), F32),
            vmem((1, B), F32),
            vmem((1, B), F32),
            dma((5,)),
            dma((3,)),
            dma((2,)),
            dma((2,)),
            dma((2, CHIPS)),
            dma((2, CHIPS)),
            dma((CHIPS,)),
            dma((CHIPS,)),
            dma((CHIPS,)),
            dma((CHIPS,)),
            dma((X * 8,)),
            dma((X * 8,)),
            dma((Z * CORE,)),
            dma((Z * CORE,)),
        ],
        compiler_params=pltpu.CompilerParams(
            collective_id=1, has_side_effects=True, vmem_limit_bytes=60 * 1024 * 1024
        ),
        name="kfac",
    )(acts, grads_out, weight_grad, old_in_factor, old_out_factor)
    update = (scale[0, 0] * nat).astype(BF16)
    return (update[None], in_factor, out_factor)


def solution(mesh):
    torus = Mesh(
        mesh.devices.reshape(X, YL, Z, YH, CORE),
        ("section_0", "section_1", "dp_0", "dp_1", "dp_2"),
    )
    in_specs = (
        P(SECTION, None, DP, None),
        P(SECTION, None, DP, None),
        P(SECTION, DP, None),
        P(SECTION, DP, None, None),
        P(SECTION, DP, None, None),
    )
    out_specs = (P(SECTION, DP, None), P(SECTION, DP, None, None), P(SECTION, DP, None, None))
    return jax.shard_map(body, mesh=torus, in_specs=in_specs, out_specs=out_specs, check_vma=False)
```

time: 234 us -> 88.1 us (0.38)
  Pallas kernels: 0 us -> 82.6 us
  waiting for transfers between devices: 76.3 us -> 0 us
  blocking collectives: 59.6 us -> 0 us
  local copies, waits for them, and re-layouts: 45.3 us -> 1.27 us
  starting transfers between devices: 27.1 us -> 0 us
  matrix products: 17.7 us -> 0 us
  between operations: 3.07 us -> 0.66 us
    pallas_call x0 -> x1, Pallas kernels: none -> 82.6 us  [body(): pl.pallas_call(kernel, out_shape=(jax.ShapeDtypeStruct((rows, width), F32...]
    all_to_all x2 -> x0, waiting for transfers between devices: 76.3 us -> none  [the longest x1 56 us: in_one_piece(): lax.all_to_all(both, axis, split_axis=split_dim, concat_axis=concat_dim,...]
    psum x5 -> x0, blocking collectives: 59.6 us -> none  [one_axis_at_a_time(): x = lax.psum(x, axis)]
    all_to_all x2 -> x0, starting transfers between devices: 27.1 us -> none  [the longest x1 17.4 us: in_one_piece(): lax.all_to_all(both, axis, split_axis=split_dim, concat_axis=concat_dim,...]
    unnamed x13 -> x6, local copies, waits for them, and re-layouts: 26.4 us -> 1.27 us
    dot_general x36 -> x0, matrix products: 17.7 us -> none  [the longest x2 5.44 us: block_gram(): jnp.einsum('tbi,tbj->bij', flat, flat, preferred_element_type=jnp.float32)]
    all_to_all x1 -> x0, local copies, waits for them, and re-layouts: 9.38 us -> none  [in_one_piece(): lax.all_to_all(both, axis, split_axis=split_dim, concat_axis=concat_dim,...]
    concatenate x1 -> x0, local copies, waits for them, and re-layouts: 7.67 us -> none  [in_one_piece(): both = jnp.concatenate(arrays, axis=along)]
  transfers between devices with their start and end apart: 2 -> 0, of which waited for: 2 -> 0; matrix products, arithmetic and copies ran while one was open for 3% -> 0% of each run, Pallas kernels for 0% -> 0%
where the time goes in v1:
time: 88.1 us; the launch traced here: 87.9 us
  Pallas kernels  82.6 us (94%)
  other arithmetic  3.42 us (4%)
  local copies, waits for them, and re-layouts  1.27 us (1%)
    pallas_call x1, Pallas kernels, body(): pl.pallas_call(kernel, out_shape=(jax.ShapeDtypeStruct((rows, width), F32...  82.6 us
    broadcast_in_dim x1, other arithmetic, body(): return (update[None], in_factor, out_factor)  3.42 us

profile of v1, /device:TPU:1, one launch (start us, length us, event | category | flops | bytes accessed | tf_op | source)
XLA Modules:
  0.0 87.9 jit_solution(7457441369689422596)
XLA Ops:
  0.6 82.6 %kfac.1 = (f32[128,4096]{1,0:T(8,128)}, f32[1,1,128,128]{3,2,1,0:T(8,128)}, f32[1,1,128,128]{3,2,1,0:T(8,128)}, f32[1,128]{1,0:T(1,128)}) custom-call(bf16[1,4,32,4096]{3,2,1,0:T(8,128)(2,1)} %acts.1, bf16[1,4,32,4096]{3,2,1,0:T(8,128)(2,1)} %grads.1, bf16[1,128,4096]{2,1,0:T(8,128)(2,1)} %wgrad.1, f32[1,1,128,128]{3,2,1,0:T(8,128)} %old_in.1, ...), custom_call_target="tpu_custom_call" | custom-call | tf_op jit(solution)/shard_map/kfac/pallas_call | solution.py:358
  83.2 0.0 copy-start.1
  83.2 0.0 copy-start
  83.2 3.4 %fusion = bf16[1,128,4096]{2,1,0:T(8,128)(2,1)} fusion(f32[128,4096]{1,0:T(8,128)} %get-tuple-element.8, f32[]{:T(128)} %bitcast.4), kind=kLoop, calls=%fused_computation.1 | loop fusion | flops 1048576 | bytes 3145732 | tf_op jit(solution)/shard_map/broadcast_in_dim | solution.py:414
  86.6 0.0 copy-done.1
  86.6 0.6 copy.10
  87.3 0.0 copy-done
  87.3 0.6 copy.11
Async XLA Ops:
  83.2 3.4 %copy-start.1 = (f32[1,1,128,128]{3,2,1,0:T(8,128)S(1)}, f32[1,1,128,128]{3,2,1,0:T(8,128)}, u32[]{:S(2)}) copy-start(f32[1,1,128,128]{3,2,1,0:T(8,128)} %get-tuple-element.15) | copy-start | bytes 196612
  83.2 4.1 %copy-start = (f32[1,1,128,128]{3,2,1,0:T(8,128)S(1)}, f32[1,1,128,128]{3,2,1,0:T(8,128)}, u32[]{:S(2)}) copy-start(f32[1,1,128,128]{3,2,1,0:T(8,128)} %get-tuple-element.16) | copy-start | bytes 196612

commit v2 on v0

v2 whole, which is shorter than its diff:
```python
import jax
import jax.numpy as jnp
from jax import lax
from jax.experimental import pallas as pl
from jax.experimental.pallas import tpu as pltpu
from jax.sharding import Mesh
from jax.sharding import PartitionSpec as P

ITERS = 8
SECTION = ("section_0", "section_1")
DP = ("dp_0", "dp_1", "dp_2")
DECAY = 0.7
DAMPING = 0.1
CLIP = 0.04
HIGH = lax.Precision.HIGHEST
LOGICAL = pl.DeviceIdType.LOGICAL

X, YL, Z, YH, CORE = 4, 4, 8, 2, 2
Y = YH * YL
CHIPS = Z * YH
PEERS = CHIPS - 1
B = 128
H = B // 2
ROWS = H + 8
GROUP = 3
F32 = jnp.float32
BF16 = jnp.bfloat16


def iotas():
    return (
        lax.broadcasted_iota(jnp.int32, (H, B), 0),
        lax.broadcasted_iota(jnp.int32, (H, B), 1),
    )


def pack(full):
    r, l = iotas()
    top, low = full[:H], pltpu.roll(full[H:], H, 1)
    body = jnp.where((l < H) & (r > l), low, top)
    diag = jnp.sum(jnp.where(r == l, low, 0.0).reshape(H // 8, 8, B), axis=0)
    return body, diag


def unpack(packed):
    r, l = iotas()
    body, diag = packed[:H], packed[H:]
    turned = jnp.concatenate([body, jnp.zeros((H, B), F32)], axis=0).T
    left_t, right_t = turned[:H], turned[H:]
    top = jnp.where((l < H) & (r > l), left_t, body)
    spread = jnp.concatenate([diag] * (H // 8), axis=0)
    corner = jnp.where(r > l, body, jnp.where(r == l, spread, left_t))
    bottom = jnp.where(l < H, right_t, pltpu.roll(corner, H, 1))
    return jnp.concatenate([top, bottom], axis=0)


def eye():
    return (
        lax.broadcasted_iota(jnp.int32, (B, B), 0) == lax.broadcasted_iota(jnp.int32, (B, B), 1)
    ).astype(F32)


def dot(a, b):
    return jnp.dot(a, b, precision=HIGH, preferred_element_type=F32)


def newton(factor):
    one = eye()
    damped = factor + DAMPING * one
    inv = 1.0 / jnp.sqrt(jnp.sum(damped * damped, keepdims=True))
    rest = one - inv * damped
    approx = inv * (one + rest)
    rest = dot(rest, rest)
    for _ in range(ITERS - 2):
        both = dot(rest, jnp.concatenate([rest, approx], axis=1))
        approx = approx + both[:, B:]
        rest = both[:, :B]
    return approx + dot(rest, approx)


def offset(i):
    j = i // 2
    return 4 + ((j + 1) // 2) * (1 - 2 * (j % 2)), 1 - i % 2


def kernel(
    acts, grads, wgrad, old_in, old_out,
    nat, fi, fo, scale_o,
    tok_in, tok_out, wv, oi, oo,
    pk_in, pk_out, own_in, own_out, d2d_in, d2d_out,
    comb_in, comb_out, rx_in, rx_out,
    xd, xf, left, q1, q2, mine, mine2,
    ld, d_s, d_r, a_s, a_r, g_s, g_r, f_s, f_r, q_s, q_r,
):
    x, yl = lax.axis_index("section_0"), lax.axis_index("section_1")
    z, yh, c = lax.axis_index("dp_0"), lax.axis_index("dp_1"), lax.axis_index("dp_2")
    y = yh * YL + yl

    loads = [
        pltpu.make_async_copy(acts.at[0], tok_in, ld.at[0]),
        pltpu.make_async_copy(grads.at[0], tok_out, ld.at[1]),
        pltpu.make_async_copy(old_in.at[0, 0], oi, ld.at[2]),
        pltpu.make_async_copy(old_out.at[0, 0], oo, ld.at[3]),
        pltpu.make_async_copy(wgrad.at[0], wv, ld.at[4]),
    ]
    for copy in loads:
        copy.start()

    z_ahead = [lax.rem(z + d, Z) for d in range(Z)]
    y_ahead = [lax.rem(y + d, Y) for d in range(Y)]
    x_at = [lax.rem(x + d, X) * (YL * Z * YH * CORE) for d in range(X)]
    y_at = [lax.rem(t, YL) * (Z * YH * CORE) + lax.div(t, YL) * CORE for t in y_ahead]
    z_at = [t * (YH * CORE) for t in z_ahead]
    c_at = [c, 1 - c]

    def device(dx=0, dy=0, dz=0, dc=0):
        return x_at[dx] + y_at[dy] + z_at[dz] + c_at[dc]

    partner = device(dc=1)
    chips = [device(dy=YL * offset(i)[1], dz=offset(i)[0]) for i in range(PEERS)]
    plane = [(dx, dy) for dx in (2, 1, 3, 0) for dy in (4, 3, 5, 2, 6, 1, 7, 0)][:-1]
    column = [(dz, dc) for dz in (4, 3, 5, 2, 6, 1, 7, 0) for dc in (1, 0)][:-1]
    planes = [device(dx=dx, dy=dy) for dx, dy in plane]
    columns = [device(dz=dz, dc=dc) for dz, dc in column]
    greeted = (
        [partner]
        + chips
        + [d for d, at in zip(planes, plane, strict=True) if at != (0, YL)]
        + [d for d, at in zip(columns, column, strict=True) if at[0] and at[1]]
    )
    barrier = pltpu.get_barrier_semaphore()
    for target in greeted:
        pl.semaphore_signal(barrier, inc=1, device_id=target, device_id_type=LOGICAL)

    def chip_to(i):
        dz, dy = offset(i)
        return lax.rem(z + dz, Z) * YH + lax.rem(yh + dy, YH)

    def chip_from(i):
        dz, dy = offset(i)
        return lax.rem(z + Z - dz, Z) * YH + lax.rem(yh + dy, YH)

    def columns_of(chip, core):
        return pl.ds(pl.multiple_of((chip * CORE + core) * B, B), B)

    def grams(tok, core, out):
        @pl.loop(0, CHIPS // 4)
        def _(g):
            for u in range(4):
                i = g * 4 + u
                t = tok[:, :, columns_of(chip_to(i), core)].reshape(B, B)
                full = lax.dot_general(
                    t, t, (((0,), (0,)), ((), ())), preferred_element_type=F32
                )
                body, diag = pack(full)
                out[i, :H] = body.astype(out.dtype)
                out[i, H:] = diag.astype(out.dtype)

    def remote(src, dst, send, recv, target):
        return pltpu.make_async_remote_copy(
            src_ref=src, dst_ref=dst, send_sem=send, recv_sem=recv,
            device_id=target, device_id_type=LOGICAL,
        )

    def combine(kind, own, got, comb, rx):
        for i in range(PEERS):
            comb[i] = (own[i] + got[i].astype(F32)).astype(BF16)
            remote(comb.at[i], rx.at[i], a_s.at[kind], a_r.at[kind], chips[i]).start()

    def whole(ref, sem):
        return pltpu.make_async_copy(ref, ref, sem)

    def collect(kind, own, got, rx):
        acc = own[PEERS] + got[PEERS].astype(F32)
        whole(rx, a_r.at[kind]).wait()
        for i in range(PEERS):
            acc = acc + rx[i].astype(F32)
        return acc

    count = F32(4.0 * 32 * Z * YH * CORE)

    loads[0].wait()
    grams(tok_in, 1 - c, pk_in)
    pl.semaphore_wait(barrier, len(greeted))
    in_pair = remote(pk_in, d2d_in, d_s.at[0], d_r.at[0], partner)
    in_pair.start()
    grams(tok_in, c, own_in)
    in_pair.wait_recv()
    combine(0, own_in, d2d_in, comb_in, rx_in)
    loads[1].wait()
    grams(tok_out, 1 - c, pk_out)
    out_pair = remote(pk_out, d2d_out, d_s.at[1], d_r.at[1], partner)
    out_pair.start()
    grams(tok_out, c, own_out)
    out_pair.wait_recv()
    combine(1, own_out, d2d_out, comb_out, rx_out)
    for copy in loads[2:]:
        copy.wait()

    gram_in = unpack(collect(0, own_in, d2d_in, rx_in))
    in_factor = DECAY * oi[...] + ((1.0 - DECAY) / count) * gram_in
    fi[...] = in_factor
    body, diag = pack(newton(in_factor))
    xd[PEERS, :H] = body.astype(BF16)
    xd[PEERS, H:] = diag.astype(BF16)

    def gather(i):
        return remote(xd.at[PEERS], xd.at[i], g_s, g_r.at[i], partner)

    def forward(i):
        return remote(xd.at[i], xf.at[i], f_s, f_r.at[i], partner)

    for i in range(PEERS):
        remote(xd.at[PEERS], xd.at[i], g_s, g_r.at[i], chips[i]).start()
    forward(PEERS).start()

    gram_out = unpack(collect(1, own_out, d2d_out, rx_out))
    out_factor = DECAY * oo[...] + ((1.0 - DECAY) / count) * gram_out
    fo[...] = out_factor
    out_inverse = newton(out_factor).astype(BF16)

    @pl.loop(0, 2)
    def _(k):
        for u in range(4):
            at = pl.ds(pl.multiple_of(k * 2048 + u * 512, 512), 512)
            left[:, at] = jnp.dot(out_inverse, wv[:, at], preferred_element_type=F32).astype(BF16)

    def block(packed, i, core, acc):
        inverse = unpack(packed[i].astype(F32)).astype(BF16)
        at = columns_of(chip_from(i), core)
        part = jnp.dot(left[:, at], inverse, preferred_element_type=F32)
        nat[:, at] = part
        part = part * wv[:, at].astype(F32)
        return acc + jnp.sum(part.reshape(B // 8, 8, B), axis=0)

    def arrivals(g):
        these = [PEERS - 1 - g * GROUP - u for u in range(GROUP)]
        for i in these:
            gather(i).wait_recv()
            forward(i).start()
        return these

    acc = block(xd, PEERS, c, jnp.zeros((8, B), F32))
    forward(PEERS).wait_recv()
    acc = block(xf, PEERS, 1 - c, acc)
    for i in arrivals(0):
        acc = block(xd, i, c, acc)

    def arrive(g, acc):
        these = arrivals(g)
        for i in these:
            forward(i + GROUP).wait_recv()
        for i in these:
            acc = block(xd, i, c, acc)
            acc = block(xf, i + GROUP, 1 - c, acc)
        return acc

    acc = lax.fori_loop(1, PEERS // GROUP, arrive, acc)
    for i in range(GROUP):
        forward(i).wait_recv()
    for i in range(GROUP):
        acc = block(xf, i, 1 - c, acc)

    mine[...] = jnp.full((1, B), jnp.sum(acc), F32)
    for k, target in enumerate(planes):
        remote(mine, q1.at[k], q_s.at[0], q_r.at[0], target).start()
    whole(q1, q_r.at[0]).wait()
    quad = mine[...] + jnp.sum(q1[...], axis=0)
    mine2[...] = quad
    for k, target in enumerate(columns):
        remote(mine2, q2.at[k], q_s.at[1], q_r.at[1], target).start()
    whole(q2, q_r.at[1]).wait()
    quad = quad + jnp.sum(q2[...], axis=0)
    numel = F32(X * YL * 4096.0 * 4096.0)
    scale_o[...] = jnp.minimum(1.0, jnp.sqrt(CLIP * numel / quad))

    in_pair.wait_send()
    out_pair.wait_send()
    whole(comb_in, a_s.at[0]).wait()
    whole(comb_out, a_s.at[1]).wait()
    whole(rx_in, g_s).wait()
    whole(xf, f_s).wait()
    whole(q1, q_s.at[0]).wait()
    whole(q2, q_s.at[1]).wait()


def finish(nat, scale, in_factor, out_factor, update_o, in_o, out_o, up, sem):
    copies = [
        pltpu.make_async_copy(in_factor, in_o.at[0, 0], sem.at[0]),
        pltpu.make_async_copy(out_factor, out_o.at[0, 0], sem.at[1]),
    ]
    for copy in copies:
        copy.start()
    factor = scale[...]
    pieces, rows = 4, nat.shape[0] // 4
    for k in range(pieces):
        part = pl.ds(k * rows, rows)
        up[part] = (factor[:, :1] * nat[part]).astype(BF16)
        copy = pltpu.make_async_copy(up.at[part], update_o.at[0, part], sem.at[2 + k])
        copy.start()
        copies.append(copy)
    for copy in copies:
        copy.wait()


def body(acts, grads_out, weight_grad, old_in_factor, old_out_factor):
    rows, width = weight_grad.shape[1:]
    hbm = pl.BlockSpec(memory_space=pltpu.HBM)
    vm = pl.BlockSpec(memory_space=pltpu.VMEM)
    dma = pltpu.SemaphoreType.DMA
    vmem = pltpu.VMEM
    packed = (CHIPS, ROWS, B)
    sent = (PEERS, ROWS, B)
    operands = [
        pltpu.with_memory_space_constraint(a, pltpu.HBM)
        for a in (acts, grads_out, weight_grad, old_in_factor, old_out_factor)
    ]
    nat, in_factor, out_factor, scale = pl.pallas_call(
        kernel,
        out_shape=(
            jax.ShapeDtypeStruct((rows, width), F32),
            jax.ShapeDtypeStruct((B, B), F32),
            jax.ShapeDtypeStruct((B, B), F32),
            jax.ShapeDtypeStruct((1, B), F32),
        ),
        in_specs=[hbm] * 5,
        out_specs=(vm,) * 4,
        scratch_shapes=[
            vmem(acts.shape[1:], BF16),
            vmem(acts.shape[1:], BF16),
            vmem((rows, width), BF16),
            vmem((B, B), F32),
            vmem((B, B), F32),
            vmem(packed, BF16),
            vmem(packed, BF16),
            vmem(packed, F32),
            vmem(packed, F32),
            vmem(packed, BF16),
            vmem(packed, BF16),
            vmem(sent, BF16),
            vmem(sent, BF16),
            vmem(sent, BF16),
            vmem(sent, BF16),
            vmem(packed, BF16),
            vmem(packed, BF16),
            vmem((rows, width), BF16),
            vmem((X * Y - 1, 1, B), F32),
            vmem((Z * CORE - 1, 1, B), F32),
            vmem((1, B), F32),
            vmem((1, B), F32),
            dma((5,)),
            dma((2,)),
            dma((2,)),
            dma((2,)),
            dma((2,)),
            dma,
            dma((PEERS,)),
            dma,
            dma((CHIPS,)),
            dma((2,)),
            dma((2,)),
        ],
        compiler_params=pltpu.CompilerParams(
            collective_id=1, has_side_effects=True, vmem_limit_bytes=24 * 1024 * 1024
        ),
        name="kfac",
    )(*operands)
    return pl.pallas_call(
        finish,
        out_shape=(
            jax.ShapeDtypeStruct((1, rows, width), BF16),
            jax.ShapeDtypeStruct(old_in_factor.shape, F32),
            jax.ShapeDtypeStruct(old_out_factor.shape, F32),
        ),
        in_specs=[vm] * 4,
        out_specs=(hbm,) * 3,
        scratch_shapes=[vmem((rows, width), BF16), dma((6,))],
        compiler_params=pltpu.CompilerParams(vmem_limit_bytes=8 * 1024 * 1024),
        name="finish",
    )(nat, scale, in_factor, out_factor)


def solution(mesh):
    torus = Mesh(
        mesh.devices.reshape(X, YL, Z, YH, CORE),
        ("section_0", "section_1", "dp_0", "dp_1", "dp_2"),
    )
    in_specs = (
        P(SECTION, None, DP, None),
        P(SECTION, None, DP, None),
        P(SECTION, DP, None),
        P(SECTION, DP, None, None),
        P(SECTION, DP, None, None),
    )
    out_specs = (P(SECTION, DP, None), P(SECTION, DP, None, None), P(SECTION, DP, None, None))
    return jax.shard_map(body, mesh=torus, in_specs=in_specs, out_specs=out_specs, check_vma=False)
```

time: 234 us -> 60.9 us (0.26)
  waiting for transfers between devices: 76.3 us -> 0 us
  Pallas kernels: 0 us -> 60.1 us
  blocking collectives: 59.6 us -> 0 us
  local copies, waits for them, and re-layouts: 45.3 us -> 0 us
  starting transfers between devices: 27.1 us -> 0 us
  matrix products: 17.7 us -> 0 us
  other arithmetic: 3.6 us -> 0 us
  between operations: 3.07 us -> 0.64 us
    all_to_all x2 -> x0, waiting for transfers between devices: 76.3 us -> none  [the longest x1 56 us: in_one_piece(): lax.all_to_all(both, axis, split_axis=split_dim, concat_axis=concat_dim,...]
    pallas_call x0 -> x2, Pallas kernels: none -> 60.1 us  [the longest x1 59 us: body(): pl.pallas_call(kernel, out_shape=(jax.ShapeDtypeStruct((rows, width), F32...]
    psum x5 -> x0, blocking collectives: 59.6 us -> none  [one_axis_at_a_time(): x = lax.psum(x, axis)]
    all_to_all x2 -> x0, starting transfers between devices: 27.1 us -> none  [the longest x1 17.4 us: in_one_piece(): lax.all_to_all(both, axis, split_axis=split_dim, concat_axis=concat_dim,...]
    unnamed x13 -> x0, local copies, waits for them, and re-layouts: 26.4 us -> none
    dot_general x36 -> x0, matrix products: 17.7 us -> none  [the longest x2 5.44 us: block_gram(): jnp.einsum('tbi,tbj->bij', flat, flat, preferred_element_type=jnp.float32)]
    all_to_all x1 -> x0, local copies, waits for them, and re-layouts: 9.38 us -> none  [in_one_piece(): lax.all_to_all(both, axis, split_axis=split_dim, concat_axis=concat_dim,...]
    concatenate x1 -> x0, local copies, waits for them, and re-layouts: 7.67 us -> none  [in_one_piece(): both = jnp.concatenate(arrays, axis=along)]
  transfers between devices with their start and end apart: 2 -> 0, of which waited for: 2 -> 0; matrix products, arithmetic and copies ran while one was open for 3% -> 0% of each run, Pallas kernels for 0% -> 0%
where the time goes in v2:
time: 60.9 us; the launch traced here: 60.7 us
  Pallas kernels  60.1 us (99%)
  between operations  0.64 us (1%)
    pallas_call x1, Pallas kernels, body(): pl.pallas_call(kernel, out_shape=(jax.ShapeDtypeStruct((rows, width), F32...  59 us

profile of v2, /device:TPU:1, one launch (start us, length us, event | category | flops | bytes accessed | tf_op | source)
XLA Modules:
  0.0 60.7 jit_solution(1227948629602281009)
XLA Ops:
  0.6 59.0 %kfac.1 = (f32[128,4096]{1,0:T(8,128)S(1)}, f32[128,128]{1,0:T(8,128)S(1)}, f32[128,128]{1,0:T(8,128)S(1)}, f32[1,128]{1,0:T(1,128)S(1)}) custom-call(bf16[1,4,32,4096]{3,2,1,0:T(8,128)(2,1)} %acts.1, bf16[1,4,32,4096]{3,2,1,0:T(8,128)(2,1)} %grads.1, bf16[1,128,4096]{2,1,0:T(8,128)(2,1)} %wgrad.1, f32[1,1,128,128]{3,2,1,0:T(8,128)} %old_in.1, ...), custom_call_target="tpu_custom_call" | custom-call | tf_op jit(solution)/shard_map/kfac/pallas_call | solution.py:318
  59.6 1.1 %finish.1 = (bf16[1,128,4096]{2,1,0:T(8,128)(2,1)}, f32[1,1,128,128]{3,2,1,0:T(8,128)}, f32[1,1,128,128]{3,2,1,0:T(8,128)}) custom-call(f32[128,4096]{1,0:T(8,128)S(1)} %get-tuple-element.7.nat, f32[1,128]{1,0:T(1,128)S(1)} %get-tuple-element.8.scale, f32[128,128]{1,0:T(8,128)S(1)} %get-tuple-element.9.in_factor, f32[128,128]{1,0:T(8,128)S(1)} %get-tuple-element.10.out_factor), custom_call_target="tpu_custom_call" | custom-call | tf_op jit(solution)/shard_map/finish/pallas_call | solution.py:368

commit v3 on v2

--- a/solution.py
+++ b/solution.py
@@ -22,7 +22,8 @@
 B = 128
 H = B // 2
 ROWS = H + 8
-GROUP = 3
+SENT = H + 2
+GROUP = 5
 F32 = jnp.float32
 BF16 = jnp.bfloat16
 
@@ -38,18 +39,17 @@
     r, l = iotas()
     top, low = full[:H], pltpu.roll(full[H:], H, 1)
     body = jnp.where((l < H) & (r > l), low, top)
-    diag = jnp.sum(jnp.where(r == l, low, 0.0).reshape(H // 8, 8, B), axis=0)
-    return body, diag
+    diag = jnp.sum(jnp.where(r == l, low, 0.0), axis=0, keepdims=True)
+    return body, jnp.broadcast_to(diag, (ROWS - H, B))
 
 
 def unpack(packed):
     r, l = iotas()
-    body, diag = packed[:H], packed[H:]
+    body, diag = packed[:H], packed[H : H + 1]
     turned = jnp.concatenate([body, jnp.zeros((H, B), F32)], axis=0).T
     left_t, right_t = turned[:H], turned[H:]
     top = jnp.where((l < H) & (r > l), left_t, body)
-    spread = jnp.concatenate([diag] * (H // 8), axis=0)
-    corner = jnp.where(r > l, body, jnp.where(r == l, spread, left_t))
+    corner = jnp.where(r > l, body, jnp.where(r == l, diag, left_t))
     bottom = jnp.where(l < H, right_t, pltpu.roll(corner, H, 1))
     return jnp.concatenate([top, bottom], axis=0)
 
@@ -60,8 +60,16 @@
     ).astype(F32)
 
 
+def parts(a):
+    high = a.astype(BF16)
+    return high, (a - high.astype(F32)).astype(BF16)
+
+
 def dot(a, b):
-    return jnp.dot(a, b, precision=HIGH, preferred_element_type=F32)
+    (ah, al), (bh, bl) = parts(a), parts(b)
+    left = jnp.concatenate([ah, ah, al], axis=1)
+    right = jnp.concatenate([bh, bl, bh], axis=0)
+    return jnp.dot(left, right, preferred_element_type=F32)
 
 
 def newton(factor):
@@ -79,8 +87,8 @@
 
 
 def offset(i):
-    j = i // 2
-    return 4 + ((j + 1) // 2) * (1 - 2 * (j % 2)), 1 - i % 2
+    j = i % Z
+    return 4 + ((j + 1) // 2) * (1 - 2 * (j % 2)), 1 - i // Z
 
 
 def kernel(
@@ -162,42 +170,60 @@
             device_id=target, device_id_type=LOGICAL,
         )
 
-    def combine(kind, own, got, comb, rx):
-        for i in range(PEERS):
+    def sent(ref, at):
+        return ref.at[at, pl.ds(0, SENT)]
+
+    def combine(kind, own, got, comb, rx, these):
+        for i in these:
             comb[i] = (own[i] + got[i].astype(F32)).astype(BF16)
-            remote(comb.at[i], rx.at[i], a_s.at[kind], a_r.at[kind], chips[i]).start()
+            landed = a_r.at[kind, i // Z]
+            remote(sent(comb, i), sent(rx, i), a_s.at[kind], landed, chips[i]).start()
 
     def whole(ref, sem):
         return pltpu.make_async_copy(ref, ref, sem)
 
-    def collect(kind, own, got, rx):
-        acc = own[PEERS] + got[PEERS].astype(F32)
-        whole(rx, a_r.at[kind]).wait()
-        for i in range(PEERS):
+    def collect(kind, side, rx, acc):
+        these = (range(Z), range(Z, PEERS))[side]
+        whole(sent(rx, pl.ds(these[0], len(these))), a_r.at[kind, side]).wait()
+        for i in these:
             acc = acc + rx[i].astype(F32)
         return acc
 
+    def mine_of(own, got):
+        return own[PEERS] + got[PEERS].astype(F32)
+
+    def halves(kind, src, dst):
+        return [
+            remote(sent(src, half), sent(dst, half), d_s.at[kind, h], d_r.at[kind, h], partner)
+            for h, half in enumerate((pl.ds(0, Z), pl.ds(Z, Z)))
+        ]
+
     count = F32(4.0 * 32 * Z * YH * CORE)
 
     loads[0].wait()
     grams(tok_in, 1 - c, pk_in)
+    grams(tok_in, c, own_in)
     pl.semaphore_wait(barrier, len(greeted))
-    in_pair = remote(pk_in, d2d_in, d_s.at[0], d_r.at[0], partner)
-    in_pair.start()
-    grams(tok_in, c, own_in)
-    in_pair.wait_recv()
-    combine(0, own_in, d2d_in, comb_in, rx_in)
+    in_pair = halves(0, pk_in, d2d_in)
+    for half in in_pair:
+        half.start()
     loads[1].wait()
     grams(tok_out, 1 - c, pk_out)
-    out_pair = remote(pk_out, d2d_out, d_s.at[1], d_r.at[1], partner)
-    out_pair.start()
+    out_pair = halves(1, pk_out, d2d_out)
+    for half in out_pair:
+        half.start()
+    in_pair[0].wait_recv()
+    combine(0, own_in, d2d_in, comb_in, rx_in, range(Z))
+    in_pair[1].wait_recv()
+    combine(0, own_in, d2d_in, comb_in, rx_in, range(Z, PEERS))
     grams(tok_out, c, own_out)
-    out_pair.wait_recv()
-    combine(1, own_out, d2d_out, comb_out, rx_out)
+    for half in out_pair:
+        half.wait_recv()
     for copy in loads[2:]:
         copy.wait()
-
-    gram_in = unpack(collect(0, own_in, d2d_in, rx_in))
+    combine(1, own_out, d2d_out, comb_out, rx_out, range(PEERS))
+    in_sum = collect(0, 1, rx_in, mine_of(own_in, d2d_in))
+    gram_in = unpack(collect(0, 0, rx_in, in_sum))
     in_factor = DECAY * oi[...] + ((1.0 - DECAY) / count) * gram_in
     fi[...] = in_factor
     body, diag = pack(newton(in_factor))
@@ -205,16 +231,17 @@
     xd[PEERS, H:] = diag.astype(BF16)
 
     def gather(i):
-        return remote(xd.at[PEERS], xd.at[i], g_s, g_r.at[i], partner)
+        return remote(sent(xd, PEERS), sent(xd, i), g_s, g_r.at[i], partner)
 
     def forward(i):
-        return remote(xd.at[i], xf.at[i], f_s, f_r.at[i], partner)
+        return remote(sent(xd, i), sent(xf, i), f_s, f_r.at[i], partner)
 
     for i in range(PEERS):
-        remote(xd.at[PEERS], xd.at[i], g_s, g_r.at[i], chips[i]).start()
+        remote(sent(xd, PEERS), sent(xd, i), g_s, g_r.at[i], chips[i]).start()
     forward(PEERS).start()
 
-    gram_out = unpack(collect(1, own_out, d2d_out, rx_out))
+    out_sum = collect(1, 1, rx_out, mine_of(own_out, d2d_out))
+    gram_out = unpack(collect(1, 0, rx_out, out_sum))
     out_factor = DECAY * oo[...] + ((1.0 - DECAY) / count) * gram_out
     fo[...] = out_factor
     out_inverse = newton(out_factor).astype(BF16)
@@ -233,33 +260,26 @@
         part = part * wv[:, at].astype(F32)
         return acc + jnp.sum(part.reshape(B // 8, 8, B), axis=0)
 
-    def arrivals(g):
+    def direct(g, acc):
         these = [PEERS - 1 - g * GROUP - u for u in range(GROUP)]
         for i in these:
             gather(i).wait_recv()
             forward(i).start()
-        return these
+        for i in these:
+            acc = block(xd, i, c, acc)
+        return acc
+
+    def forwarded(g, acc):
+        these = [PEERS - g * 4 - u for u in range(4)]
+        for i in these:
+            forward(i).wait_recv()
+        for i in these:
+            acc = block(xf, i, 1 - c, acc)
+        return acc
 
     acc = block(xd, PEERS, c, jnp.zeros((8, B), F32))
-    forward(PEERS).wait_recv()
-    acc = block(xf, PEERS, 1 - c, acc)
-    for i in arrivals(0):
-        acc = block(xd, i, c, acc)
-
-    def arrive(g, acc):
-        these = arrivals(g)
-        for i in these:
-            forward(i + GROUP).wait_recv()
-        for i in these:
-            acc = block(xd, i, c, acc)
-            acc = block(xf, i + GROUP, 1 - c, acc)
-        return acc
-
-    acc = lax.fori_loop(1, PEERS // GROUP, arrive, acc)
-    for i in range(GROUP):
-        forward(i).wait_recv()
-    for i in range(GROUP):
-        acc = block(xf, i, 1 - c, acc)
+    acc = lax.fori_loop(0, PEERS // GROUP, direct, acc)
+    acc = lax.fori_loop(0, CHIPS // 4, forwarded, acc)
 
     mine[...] = jnp.full((1, B), jnp.sum(acc), F32)
     for k, target in enumerate(planes):
@@ -274,12 +294,13 @@
     numel = F32(X * YL * 4096.0 * 4096.0)
     scale_o[...] = jnp.minimum(1.0, jnp.sqrt(CLIP * numel / quad))
 
-    in_pair.wait_send()
-    out_pair.wait_send()
-    whole(comb_in, a_s.at[0]).wait()
-    whole(comb_out, a_s.at[1]).wait()
-    whole(rx_in, g_s).wait()
-    whole(xf, f_s).wait()
+    for half in in_pair + out_pair:
+        half.wait_send()
+    every = pl.ds(0, PEERS)
+    whole(sent(comb_in, every), a_s.at[0]).wait()
+    whole(sent(comb_out, every), a_s.at[1]).wait()
+    whole(sent(rx_in, every), g_s).wait()
+    whole(sent(xf, pl.ds(0, CHIPS)), f_s).wait()
     whole(q1, q_s.at[0]).wait()
     whole(q2, q_s.at[1]).wait()
 
@@ -349,10 +370,10 @@
             vmem((1, B), F32),
             vmem((1, B), F32),
             dma((5,)),
+            dma((2, 2)),
+            dma((2, 2)),
             dma((2,)),
-            dma((2,)),
-            dma((2,)),
-            dma((2,)),
+            dma((2, 2)),
             dma,
             dma((PEERS,)),
             dma,

time: 60.9 us -> 57 us (0.936)
  Pallas kernels: 60.1 us -> 56.2 us
    pallas_call x1, Pallas kernels: 59 us -> 55.1 us  [body(): pl.pallas_call(kernel, out_shape=(jax.ShapeDtypeStruct((rows, width), F32...]
where the time goes in v3:
time: 57 us; the launch traced here: 56.9 us
  Pallas kernels  56.2 us (99%)
  between operations  0.64 us (1%)
    pallas_call x1, Pallas kernels, body(): pl.pallas_call(kernel, out_shape=(jax.ShapeDtypeStruct((rows, width), F32...  55.1 us

profile of v3, /device:TPU:1, one launch (start us, length us, event | category | flops | bytes accessed | tf_op | source)
XLA Modules:
  0.0 56.9 jit_solution(167044307587875629)
XLA Ops:
  0.6 55.1 %kfac.1 = (f32[128,4096]{1,0:T(8,128)S(1)}, f32[128,128]{1,0:T(8,128)S(1)}, f32[128,128]{1,0:T(8,128)S(1)}, f32[1,128]{1,0:T(1,128)S(1)}) custom-call(bf16[1,4,32,4096]{3,2,1,0:T(8,128)(2,1)} %acts.1, bf16[1,4,32,4096]{3,2,1,0:T(8,128)(2,1)} %grads.1, bf16[1,128,4096]{2,1,0:T(8,128)(2,1)} %wgrad.1, f32[1,1,128,128]{3,2,1,0:T(8,128)} %old_in.1, ...), custom_call_target="tpu_custom_call" | custom-call | tf_op jit(solution)/shard_map/kfac/pallas_call | solution.py:339
  55.7 1.1 %finish.1 = (bf16[1,128,4096]{2,1,0:T(8,128)(2,1)}, f32[1,1,128,128]{3,2,1,0:T(8,128)}, f32[1,1,128,128]{3,2,1,0:T(8,128)}) custom-call(f32[128,4096]{1,0:T(8,128)S(1)} %get-tuple-element.7.nat, f32[1,128]{1,0:T(1,128)S(1)} %get-tuple-element.8.scale, f32[128,128]{1,0:T(8,128)S(1)} %get-tuple-element.9.in_factor, f32[128,128]{1,0:T(8,128)S(1)} %get-tuple-element.10.out_factor), custom_call_target="tpu_custom_call" | custom-call | tf_op jit(solution)/shard_map/finish/pallas_call | solution.py:389

commit v4 on v3

--- a/solution.py
+++ b/solution.py
@@ -104,6 +104,31 @@
     z, yh, c = lax.axis_index("dp_0"), lax.axis_index("dp_1"), lax.axis_index("dp_2")
     y = yh * YL + yl
 
+    z_ahead = [lax.rem(z + d, Z) for d in range(Z)]
+    y_ahead = [lax.rem(y + d, Y) for d in range(Y)]
+    x_at = [lax.rem(x + d, X) * (YL * Z * YH * CORE) for d in range(X)]
+    y_at = [lax.rem(t, YL) * (Z * YH * CORE) + lax.div(t, YL) * CORE for t in y_ahead]
+    z_at = [t * (YH * CORE) for t in z_ahead]
+    c_at = [c, 1 - c]
+
+    def device(dx=0, dy=0, dz=0, dc=0):
+        return x_at[dx] + y_at[dy] + z_at[dz] + c_at[dc]
+
+    partner = device(dc=1)
+    chips = [device(dy=YL * offset(i)[1], dz=offset(i)[0]) for i in range(PEERS)]
+    plane = [(dx, dy) for dx in (2, 1, 3, 0) for dy in (4, 3, 5, 2, 6, 1, 7, 0)][:-1]
+    column = [(dz, dc) for dz in (4, 3, 5, 2, 6, 1, 7, 0) for dc in (1, 0)][:-1]
+    planes = [device(dx=dx, dy=dy) for dx, dy in plane]
+    columns = [device(dz=dz, dc=dc) for dz, dc in column]
+    greeted = (
+        chips
+        + [partner]
+        + [d for d, at in zip(planes, plane, strict=True) if at != (0, YL)]
+        + [d for d, at in zip(columns, column, strict=True) if at[0] and at[1]]
+    )
+    barrier = pltpu.get_barrier_semaphore()
+    for target in greeted[:PEERS]:
+        pl.semaphore_signal(barrier, inc=1, device_id=target, device_id_type=LOGICAL)
     loads = [
         pltpu.make_async_copy(acts.at[0], tok_in, ld.at[0]),
         pltpu.make_async_copy(grads.at[0], tok_out, ld.at[1]),
@@ -113,31 +138,7 @@
     ]
     for copy in loads:
         copy.start()
-
-    z_ahead = [lax.rem(z + d, Z) for d in range(Z)]
-    y_ahead = [lax.rem(y + d, Y) for d in range(Y)]
-    x_at = [lax.rem(x + d, X) * (YL * Z * YH * CORE) for d in range(X)]
-    y_at = [lax.rem(t, YL) * (Z * YH * CORE) + lax.div(t, YL) * CORE for t in y_ahead]
-    z_at = [t * (YH * CORE) for t in z_ahead]
-    c_at = [c, 1 - c]
-
-    def device(dx=0, dy=0, dz=0, dc=0):
-        return x_at[dx] + y_at[dy] + z_at[dz] + c_at[dc]
-
-    partner = device(dc=1)
-    chips = [device(dy=YL * offset(i)[1], dz=offset(i)[0]) for i in range(PEERS)]
-    plane = [(dx, dy) for dx in (2, 1, 3, 0) for dy in (4, 3, 5, 2, 6, 1, 7, 0)][:-1]
-    column = [(dz, dc) for dz in (4, 3, 5, 2, 6, 1, 7, 0) for dc in (1, 0)][:-1]
-    planes = [device(dx=dx, dy=dy) for dx, dy in plane]
-    columns = [device(dz=dz, dc=dc) for dz, dc in column]
-    greeted = (
-        [partner]
-        + chips
-        + [d for d, at in zip(planes, plane, strict=True) if at != (0, YL)]
-        + [d for d, at in zip(columns, column, strict=True) if at[0] and at[1]]
-    )
-    barrier = pltpu.get_barrier_semaphore()
-    for target in greeted:
+    for target in greeted[PEERS:]:
         pl.semaphore_signal(barrier, inc=1, device_id=target, device_id_type=LOGICAL)
 
     def chip_to(i):
@@ -221,8 +222,9 @@
         half.wait_recv()
     for copy in loads[2:]:
         copy.wait()
-    combine(1, own_out, d2d_out, comb_out, rx_out, range(PEERS))
+    combine(1, own_out, d2d_out, comb_out, rx_out, range(Z))
     in_sum = collect(0, 1, rx_in, mine_of(own_in, d2d_in))
+    combine(1, own_out, d2d_out, comb_out, rx_out, range(Z, PEERS))
     gram_in = unpack(collect(0, 0, rx_in, in_sum))
     in_factor = DECAY * oi[...] + ((1.0 - DECAY) / count) * gram_in
     fi[...] = in_factor
@@ -260,28 +262,34 @@
         part = part * wv[:, at].astype(F32)
         return acc + jnp.sum(part.reshape(B // 8, 8, B), axis=0)
 
-    def direct(g, acc):
+    def arrived(g):
         these = [PEERS - 1 - g * GROUP - u for u in range(GROUP)]
         for i in these:
             gather(i).wait_recv()
             forward(i).start()
+        return these
+
+    def both(g, acc):
+        these = arrived(g)
+        for i in these:
+            forward(i + GROUP).wait_recv()
         for i in these:
             acc = block(xd, i, c, acc)
+            acc = block(xf, i + GROUP, 1 - c, acc)
         return acc
 
-    def forwarded(g, acc):
-        these = [PEERS - g * 4 - u for u in range(4)]
-        for i in these:
-            forward(i).wait_recv()
-        for i in these:
-            acc = block(xf, i, 1 - c, acc)
-        return acc
-
     acc = block(xd, PEERS, c, jnp.zeros((8, B), F32))
-    acc = lax.fori_loop(0, PEERS // GROUP, direct, acc)
-    acc = lax.fori_loop(0, CHIPS // 4, forwarded, acc)
-
-    mine[...] = jnp.full((1, B), jnp.sum(acc), F32)
+    for i in arrived(0):
+        acc = block(xd, i, c, acc)
+    forward(PEERS).wait_recv()
+    acc = block(xf, PEERS, 1 - c, acc)
+    acc = lax.fori_loop(1, PEERS // GROUP, both, acc)
+    for i in range(GROUP):
+        forward(i).wait_recv()
+    for i in range(GROUP):
+        acc = block(xf, i, 1 - c, acc)
+
+    mine[...] = jnp.broadcast_to(jnp.sum(acc, keepdims=True), (1, B))
     for k, target in enumerate(planes):
         remote(mine, q1.at[k], q_s.at[0], q_r.at[0], target).start()
     whole(q1, q_r.at[0]).wait()

time: 57 us -> 56.4 us (0.989)
  no operation moved by 1% of the time
where the time goes in v4:
time: 56.4 us; the launch traced here: 56.3 us
  Pallas kernels  55.7 us (99%)
  between operations  0.64 us (1%)
    pallas_call x1, Pallas kernels, body(): pl.pallas_call(kernel, out_shape=(jax.ShapeDtypeStruct((rows, width), F32...  54.5 us
    pallas_call x1, Pallas kernels, body(): pl.pallas_call(finish, out_shape=(jax.ShapeDtypeStruct((1, rows, width),...  1.13 us

profile of v4, /device:TPU:1, one launch (start us, length us, event | category | flops | bytes accessed | tf_op | source)
XLA Modules:
  0.0 56.3 jit_solution(5390306506254333818)
XLA Ops:
  0.6 54.5 %kfac.1 = (f32[128,4096]{1,0:T(8,128)S(1)}, f32[128,128]{1,0:T(8,128)S(1)}, f32[128,128]{1,0:T(8,128)S(1)}, f32[1,128]{1,0:T(1,128)S(1)}) custom-call(bf16[1,4,32,4096]{3,2,1,0:T(8,128)(2,1)} %acts.1, bf16[1,4,32,4096]{3,2,1,0:T(8,128)(2,1)} %grads.1, bf16[1,128,4096]{2,1,0:T(8,128)(2,1)} %wgrad.1, f32[1,1,128,128]{3,2,1,0:T(8,128)} %old_in.1, ...), custom_call_target="tpu_custom_call" | custom-call | tf_op jit(solution)/shard_map/kfac/pallas_call | solution.py:347
  55.2 1.1 %finish.1 = (bf16[1,128,4096]{2,1,0:T(8,128)(2,1)}, f32[1,1,128,128]{3,2,1,0:T(8,128)}, f32[1,1,128,128]{3,2,1,0:T(8,128)}) custom-call(f32[128,4096]{1,0:T(8,128)S(1)} %get-tuple-element.7.nat, f32[1,128]{1,0:T(1,128)S(1)} %get-tuple-element.8.scale, f32[128,128]{1,0:T(8,128)S(1)} %get-tuple-element.9.in_factor, f32[128,128]{1,0:T(8,128)S(1)} %get-tuple-element.10.out_factor), custom_call_target="tpu_custom_call" | custom-call | tf_op jit(solution)/shard_map/finish/pallas_call | solution.py:397
